TPU v7x, 768 devices: a whole 4x8x12 slice. The times are simulated.
768 devices in a mesh: dp: 96 (over y_lo, z, x), seq: 8 (over y_hi, core).
Axes of the slice: x: 4, y: 8 (y_hi: 4, y_lo: 2; y = y_hi * 2 + y_lo), z: 12, core: 2. Of those that a mesh axis runs over, the one named last changes fastest.
Arguments:
- queries: bfloat16 [98304, 2048], P(('dp', 'seq')), may hold values from -6 to 6
- keys: bfloat16 [98304, 2048], P(('dp', 'seq')), may hold values from -6 to 6
- values: bfloat16 [98304, 2048], P(('dp', 'seq')), may hold values from -6 to 6
- q_gain: float32 [2048], replicated, may hold values from 0.25 to 1.75
- k_gain: float32 [2048], replicated, may hold values from 0.25 to 1.75
- out_grad: bfloat16 [98304, 2048], P(('dp', 'seq')), may hold values from -16 to 16
- segments: int32 [96, 1024], P('dp'), may hold values from 0 to 3, never falling along the last dimension, each value on 1 to 512 neighbouring positions
- visible: int32 [96, 1024], P('dp'), may hold values 0 or 1
Outputs:
- attn_out: bfloat16 [98304, 2048], P(('dp', 'seq'))
- query_grad: bfloat16 [98304, 2048], P(('dp', 'seq'))
- key_grad: bfloat16 [98304, 2048], P(('dp', 'seq'))
- value_grad: bfloat16 [98304, 2048], P(('dp', 'seq'))
- q_gain_grad: float32 [2048], replicated
- k_gain_grad: float32 [2048], replicated
Inputs may be any that keep to these rules, and one draw needn't show every extreme that they name: `segments`: along each packed sequence the clip numbers never fall; each of the 4 clips holds 1 to 512 slots.
All inputs are finite; a program needn't handle non-finite values. No bound on the sum of `visible` on one device may be relied on, other than what follows from the above.
Results may differ from a plain program's by a relative error of at most 0.012.
The roundings to bfloat16 on the way count: a program that leaves them out, or rounds other values in their place, can miss the bound.
Values may be sent and summed in bfloat16 or wider, within the bound.
A program may use at most 64 MiB of HBM per device.

v0:
```python
import jax
import jax.numpy as jnp
from jax import lax
from jax.sharding import Mesh
from jax.sharding import PartitionSpec as P

D_HEAD = 128
SEQ = ("seq_0", "seq_1")
DP_SEQ = ("dp_0", "dp_1", "dp_2", "seq_0", "seq_1")
DP = ("dp_0", "dp_1", "dp_2")


epsilon = 1e-06


def by_axis(value, axes):
    for axis in axes:
        value = lax.psum(value, axis)
    return value


def normalize(raw_rows, gain_vec):
    raw_f32 = raw_rows.astype(jnp.float32)
    inv_rms = lax.rsqrt(jnp.mean(raw_f32 * raw_f32, axis=-1, keepdims=True) + epsilon)
    return ((raw_f32 * inv_rms * gain_vec).astype(jnp.bfloat16), inv_rms)


def norm_back(raw_rows, inv_rms, gain_vec, grad_norm):
    raw_f32 = raw_rows.astype(jnp.float32)
    grad_f32 = grad_norm.astype(jnp.float32)
    scaled_grad = gain_vec * grad_f32
    mean_term = jnp.mean(scaled_grad * raw_f32, axis=-1, keepdims=True)
    grad_raw = inv_rms * scaled_grad - raw_f32 * inv_rms**3 * mean_term
    return (grad_raw.astype(jnp.bfloat16), jnp.sum(grad_f32 * raw_f32 * inv_rms, axis=0))


def attend(q_norm, k_norm, val_rows, grad_rows, seg_row, vis_row, keep_out):
    seq_rows, feature_count = q_norm.shape
    head_count = feature_count // D_HEAD
    score_scale = D_HEAD ** (-0.5)
    block_rows = 512
    block_count = seq_rows // block_rows
    k_three = k_norm.reshape(seq_rows, head_count, D_HEAD)
    v_three = val_rows.reshape(seq_rows, head_count, D_HEAD)
    positions = jnp.arange(seq_rows, dtype=jnp.int32)
    key_open = vis_row == 1

    def one_block(totals, block_index):
        block_start = block_index * block_rows
        q_block = lax.dynamic_slice_in_dim(q_norm, block_start, block_rows, 0).reshape(
            block_rows, head_count, D_HEAD
        )
        seg_block = lax.dynamic_slice_in_dim(seg_row, block_start, block_rows, 0)
        pos_block = block_start + jnp.arange(block_rows, dtype=jnp.int32)
        allowed = (seg_block[:, None] == seg_row[None, :]) & (
            key_open[None, :] | (pos_block[:, None] == positions[None, :])
        )
        scores = (
            jnp.einsum("shd,thd->hst", q_block, k_three, preferred_element_type=jnp.float32)
            * score_scale
        )
        scores = jnp.where(allowed[None], scores, -1e30)
        row_max = jnp.max(scores, axis=-1, keepdims=True)
        weights = jnp.exp(scores - row_max)
        attn_prob = weights / jnp.sum(weights, axis=-1, keepdims=True)
        prob_half = attn_prob.astype(jnp.bfloat16)
        block_out = jnp.zeros((block_rows, feature_count), jnp.bfloat16)
        if keep_out:
            block_out = (
                jnp.einsum("hst,thd->shd", prob_half, v_three, preferred_element_type=jnp.float32)
                .reshape(block_rows, feature_count)
                .astype(jnp.bfloat16)
            )
        if grad_rows is None:
            return (totals, (block_out, block_out))
        grad_block = lax.dynamic_slice_in_dim(grad_rows, block_start, block_rows, 0).reshape(
            block_rows, head_count, D_HEAD
        )
        dprob = jnp.einsum("shd,thd->hst", grad_block, v_three, preferred_element_type=jnp.float32)
        value_add = jnp.einsum(
            "hst,shd->thd", prob_half, grad_block, preferred_element_type=jnp.float32
        )
        row_dot = jnp.sum(attn_prob * dprob, axis=-1, keepdims=True)
        score_grad = (attn_prob * (dprob - row_dot) * score_scale).astype(jnp.bfloat16)
        q_grad = (
            jnp.einsum("hst,thd->shd", score_grad, k_three, preferred_element_type=jnp.float32)
            .reshape(block_rows, feature_count)
            .astype(jnp.bfloat16)
        )
        key_add = jnp.einsum(
            "hst,shd->thd", score_grad, q_block, preferred_element_type=jnp.float32
        )
        return ((totals[0] + key_add, totals[1] + value_add), (block_out, q_grad))

    empty = jnp.zeros((seq_rows, head_count, D_HEAD), jnp.float32)
    totals, stacked = lax.scan(one_block, (empty, empty), jnp.arange(block_count, dtype=jnp.int32))
    attn_out = stacked[0].reshape(seq_rows, feature_count)
    if grad_rows is None:
        return attn_out
    q_grad = stacked[1].reshape(seq_rows, feature_count)
    k_grad = totals[0].reshape(seq_rows, feature_count).astype(jnp.bfloat16)
    v_grad = totals[1].reshape(seq_rows, feature_count).astype(jnp.bfloat16)
    return (attn_out, q_grad, k_grad, v_grad)


def per_device(queries, keys, values, q_gain, k_gain, out_grad, segments, visible):
    q_norm, q_inv = normalize(queries, q_gain)
    k_norm, k_inv = normalize(keys, k_gain)
    seg_row = segments[0]
    vis_row = visible[0]
    query_heads, key_heads, value_heads = (
        lax.all_to_all(q_norm, SEQ, split_axis=1, concat_axis=0, tiled=True),
        lax.all_to_all(k_norm, SEQ, split_axis=1, concat_axis=0, tiled=True),
        lax.all_to_all(values, SEQ, split_axis=1, concat_axis=0, tiled=True),
    )
    out_part = attend(query_heads, key_heads, value_heads, None, seg_row, vis_row, True)
    attn_out = lax.all_to_all(out_part, SEQ, split_axis=0, concat_axis=1, tiled=True)
    grad_heads = lax.all_to_all(out_grad, SEQ, split_axis=1, concat_axis=0, tiled=True)
    unused_out, q_part, k_part, v_part = attend(
        query_heads, key_heads, value_heads, grad_heads, seg_row, vis_row, False
    )
    q_grad, k_grad, value_grad = (
        lax.all_to_all(q_part, SEQ, split_axis=0, concat_axis=1, tiled=True),
        lax.all_to_all(k_part, SEQ, split_axis=0, concat_axis=1, tiled=True),
        lax.all_to_all(v_part, SEQ, split_axis=0, concat_axis=1, tiled=True),
    )
    query_grad, q_gain_part = norm_back(queries, q_inv, q_gain, q_grad)
    key_grad, k_gain_part = norm_back(keys, k_inv, k_gain, k_grad)
    q_gain_grad, k_gain_grad = (by_axis(q_gain_part, DP_SEQ), by_axis(k_gain_part, DP_SEQ))
    return (attn_out, query_grad, key_grad, value_grad, q_gain_grad, k_gain_grad)


def solution(mesh):
    finer = Mesh(mesh.devices.reshape(2, 12, 4, 4, 2), ("dp_0", "dp_1", "dp_2", "seq_0", "seq_1"))
    placed = (
        P(DP_SEQ, None),
        P(DP_SEQ, None),
        P(DP_SEQ, None),
        P(),
        P(),
        P(DP_SEQ, None),
        P(DP, None),
        P(DP, None),
    )
    return jax.shard_map(
        per_device,
        mesh=finer,
        in_specs=placed,
        out_specs=(P(DP_SEQ, None), P(DP_SEQ, None), P(DP_SEQ, None), P(DP_SEQ, None), P(), P()),
        check_vma=False,
    )
```

profile of v0, /device:TPU:1, one launch (start us, length us, event | category | flops | bytes accessed | tf_op | source)
XLA Modules:
  0.0 350.5 jit_solution(1463303425104042173)
XLA Ops:
  0.7 1.4 copy.83
  2.4 1.0 fusion.72
  4.4 14.0 %all-to-all-start.1 = ((bf16[128,8,256]{2,0,1:T(8,128)(2,1)}), bf16[128,8,256]{2,0,1:T(8,128)(2,1)S(1)}, u32[]{:S(2)}, u32[]{:S(2)}) async-start(bf16[128,8,256]{2,0,1:T(8,128)(2,1)} %copy.84), calls=%async_computation.1 | async-start | bytes 1048576 | tf_op jit(solution)/shard_map/all_to_all | solution.py:113
  19.4 12.1 %all-to-all-done.1 = bf16[128,8,256]{2,0,1:T(8,128)(2,1)S(1)} async-done(((bf16[128,8,256]{2,0,1:T(8,128)(2,1)}), bf16[128,8,256]{2,0,1:T(8,128)(2,1)S(1)}, u32[]{:S(2)}, u32[]{:S(2)}) %all-to-all-start.1) | async-done | bytes 524320 | tf_op jit(solution)/shard_map/all_to_all | solution.py:113
  31.5 5.9 %all-to-all-start.2 = ((bf16[128,8,256]{0,2,1:T(8,128)(2,1)}), bf16[128,8,256]{0,2,1:T(8,128)(2,1)S(1)}, u32[]{:S(2)}, u32[]{:S(2)}) async-start(bf16[128,8,256]{0,2,1:T(8,128)(2,1)} %bitcast.5), calls=%async_computation.2 | async-start | bytes 1048576 | tf_op jit(solution)/shard_map/all_to_all | solution.py:114
  38.0 1.1 fusion.63
  39.1 13.4 %all-to-all-done.2 = bf16[128,8,256]{0,2,1:T(8,128)(2,1)S(1)} async-done(((bf16[128,8,256]{0,2,1:T(8,128)(2,1)}), bf16[128,8,256]{0,2,1:T(8,128)(2,1)S(1)}, u32[]{:S(2)}, u32[]{:S(2)}) %all-to-all-start.2) | async-done | bytes 524320 | tf_op jit(solution)/shard_map/all_to_all | solution.py:114
  52.5 3.8 %all-to-all-start = ((bf16[128,8,256]{0,2,1:T(8,128)(2,1)}), bf16[128,8,256]{0,2,1:T(8,128)(2,1)S(1)}, u32[]{:S(2)}, u32[]{:S(2)}) async-start(bf16[128,8,256]{0,2,1:T(8,128)(2,1)} %bitcast.1), calls=%async_computation | async-start | bytes 1048576 | tf_op jit(solution)/shard_map/all_to_all | solution.py:112
  56.3 2.1 copy.90
  59.7 1.0 reshape.297
  60.8 9.7 %all-to-all-done = bf16[128,8,256]{0,2,1:T(8,128)(2,1)S(1)} async-done(((bf16[128,8,256]{0,2,1:T(8,128)(2,1)}), bf16[128,8,256]{0,2,1:T(8,128)(2,1)S(1)}, u32[]{:S(2)}, u32[]{:S(2)}) %all-to-all-start) | async-done | bytes 524320 | tf_op jit(solution)/shard_map/all_to_all | solution.py:112
  70.5 7.3 %all-to-all-start.4 = ((bf16[128,8,256]{0,2,1:T(8,128)(2,1)}), bf16[128,8,256]{0,2,1:T(8,128)(2,1)S(1)}, u32[]{:S(2)}, u32[]{:S(2)}) async-start(bf16[128,8,256]{0,2,1:T(8,128)(2,1)} %bitcast.10), calls=%async_computation.4 | async-start | bytes 1048576 | tf_op jit(solution)/shard_map/all_to_all | solution.py:118
  78.7 21.6 %while.26 = (s32[]{:T(128)}, bf16[2,512,256]{2,1,0:T(8,128)(2,1)}, s32[2]{0:T(128)S(1)}, s32[1024]{0:T(1024)S(1)}, s32[1,1024]{1,0:T(1,128)S(1)}, /*index=5*/pre...) while((s32[]{:T(128)}, bf16[2,512,256]{2,1,0:T(8,128)(2,1)}, ...), condition=%wide.region_5.6_spmd.clone, body=%wide.region_2.5_spmd.clone.sunk | while | flops 545392128 | bytes 12606671 | solution.py:96
  80.7 4.7 %fusion.124 = (f32[2,512]{1,0:T(2,128)S(1)}, f32[2,512,1024]{2,1,0:T(8,128)}) fusion(pred[512,1024]{1,0:T(8,128)(4,1)S(1)} %fusion.123, bf16[512,2,128]{0,2,1:T(8,128)(2,1)S(1)} %bitcast.136, bf16[1024,2,128]{2,0,1:T(8,128)(2,1)} %get-tuple-element.536), kind=kOutput, calls=%fused_computation.98.clone.1 | convolution fusion | flops 272630784 | bytes 5509120 | tf_op jit(solution)/shard_map/while/body/eval_jaxpr/sub | solution.py:64
  85.4 3.2 fusion.125
  91.5 4.7 %fusion.124 = (f32[2,512]{1,0:T(2,128)S(1)}, f32[2,512,1024]{2,1,0:T(8,128)}) fusion(pred[512,1024]{1,0:T(8,128)(4,1)S(1)} %fusion.123, bf16[512,2,128]{0,2,1:T(8,128)(2,1)S(1)} %bitcast.136, bf16[1024,2,128]{2,0,1:T(8,128)(2,1)} %get-tuple-element.536), kind=kOutput, calls=%fused_computation.98.clone.1 | convolution fusion | flops 272630784 | bytes 5509120 | tf_op jit(solution)/shard_map/while/body/eval_jaxpr/sub | solution.py:64
  96.3 3.2 fusion.125
  100.3 1.1 copy.92
  101.4 1.3 copy.94
  102.8 7.2 %all-to-all-start.3 = ((bf16[8,128,256]{2,1,0:T(8,128)(2,1)}), bf16[8,128,256]{2,1,0:T(8,128)(2,1)}, u32[]{:S(2)}, u32[]{:S(2)}) async-start(bf16[8,128,256]{2,1,0:T(8,128)(2,1)} %bitcast.144), calls=%async_computation.3 | async-start | bytes 1048576 | tf_op jit(solution)/shard_map/all_to_all | solution.py:117
  111.8 73.4 %while.27 = (s32[]{:T(128)}, f32[1024,2,128]{0,2,1:T(8,128)}, f32[1024,2,128]{0,2,1:T(8,128)}, bf16[2,512,256]{2,1,0:T(8,128)(2,1)}, s32[2]{0:T(128)S(1)}, /*ind...) while((s32[]{:T(128)}, f32[1024,2,128]{0,2,1:T(8,128)}, ...), condition=%wide.region_10.11_spmd.clone, body=%wide.region_6.10_spmd.clone.sunk | while | flops 1366431232 | bytes 46431560 | solution.py:96
  115.0 4.7 %fusion.138 = (f32[2,512]{1,0:T(2,128)S(1)}, f32[2,512,1024]{2,1,0:T(8,128)}) fusion(pred[512,1024]{1,0:T(8,128)(4,1)S(1)} %fusion.137, bf16[512,2,128]{0,2,1:T(8,128)(2,1)S(1)} %bitcast.134, bf16[1024,2,128]{0,2,1:T(8,128)(2,1)} %get-tuple-element.583), kind=kOutput, calls=%fused_computation.99.clone.1 | convolution fusion | flops 272630784 | bytes 5509120 | tf_op jit(solution)/shard_map/while/body/eval_jaxpr/sub | solution.py:64
  119.7 3.7 %fusion.140 = f32[1024,2,128]{0,2,1:T(8,128)} fusion(bf16[512,2,128]{0,2,1:T(8,128)(2,1)S(1)} %bitcast.132, f32[1024,2,128]{0,2,1:T(8,128)} %get-tuple-element.560, pred[]{:T(512)S(6)} %compare.3, f32[2,512,1024]{2,1,0:T(8,128)} %get-tuple-element.501, f32[2,512]{1,0:T(2,128)S(1)} %get-tuple-element.502), kind=kOutput, calls=%fused_computation.44.clone.1 | convolution fusion | flops 271056896 | bytes 6557697 | tf_op jit(solution)/shard_map/while/body/eval_jaxpr/hst,shd->thd/dot_general | solution.py:80
  123.4 2.7 fusion.136
  126.1 11.2 %fusion.141 = bf16[2,512,128]{1,2,0:T(8,128)(2,1)S(1)} fusion(bf16[1024,2,128]{0,2,1:T(8,128)(2,1)S(1)} %copy-done.6, f32[2,512,1024]{2,1,0:T(8,128)} %fusion.136, f32[2,512,1024]{2,1,0:T(8,128)} %get-tuple-element.501, f32[2,512]{1,0:T(2,128)S(1)} %get-tuple-element.502), kind=kOutput, calls=%fused_computation.46.clone.1 | convolution fusion | flops 275908608 | bytes 9179136 | tf_op jit(solution)/shard_map/while/body/eval_jaxpr/hst,thd->shd/dot_general | solution.py:86
  137.4 10.0 %fusion.139 = f32[1024,2,128]{0,2,1:T(8,128)} fusion(bf16[512,2,128]{0,2,1:T(8,128)(2,1)S(1)} %bitcast.135, f32[2,512,1024]{2,1,0:T(8,128)} %fusion.136, f32[1024,2,128]{0,2,1:T(8,128)} %get-tuple-element.559, pred[]{:T(512)S(6)} %compare.3, f32[2,512,1024]{2,1,0:T(8,128)} %get-tuple-element.501, f32[2,512]{1,0:T(2,128)S(1)} %get-tuple-element.502), kind=kOutput, calls=%fused_computation.45.clone.1 | convolution fusion | flops 276301824 | bytes 10752001 | tf_op jit(solution)/shard_map/while/body/eval_jaxpr/hst,shd->thd/dot_general | solution.py:90
  151.5 4.7 %fusion.138 = (f32[2,512]{1,0:T(2,128)S(1)}, f32[2,512,1024]{2,1,0:T(8,128)}) fusion(pred[512,1024]{1,0:T(8,128)(4,1)S(1)} %fusion.137, bf16[512,2,128]{0,2,1:T(8,128)(2,1)S(1)} %bitcast.134, bf16[1024,2,128]{0,2,1:T(8,128)(2,1)} %get-tuple-element.583), kind=kOutput, calls=%fused_computation.99.clone.1 | convolution fusion | flops 272630784 | bytes 5509120 | tf_op jit(solution)/shard_map/while/body/eval_jaxpr/sub | solution.py:64
  156.1 4.0 %fusion.140 = f32[1024,2,128]{0,2,1:T(8,128)} fusion(bf16[512,2,128]{0,2,1:T(8,128)(2,1)S(1)} %bitcast.132, f32[1024,2,128]{0,2,1:T(8,128)} %get-tuple-element.560, pred[]{:T(512)S(6)} %compare.3, f32[2,512,1024]{2,1,0:T(8,128)} %get-tuple-element.501, f32[2,512]{1,0:T(2,128)S(1)} %get-tuple-element.502), kind=kOutput, calls=%fused_computation.44.clone.1 | convolution fusion | flops 271056896 | bytes 6557697 | tf_op jit(solution)/shard_map/while/body/eval_jaxpr/hst,shd->thd/dot_general | solution.py:80
  160.2 2.7 fusion.136
  162.9 11.2 %fusion.141 = bf16[2,512,128]{1,2,0:T(8,128)(2,1)S(1)} fusion(bf16[1024,2,128]{0,2,1:T(8,128)(2,1)S(1)} %copy-done.6, f32[2,512,1024]{2,1,0:T(8,128)} %fusion.136, f32[2,512,1024]{2,1,0:T(8,128)} %get-tuple-element.501, f32[2,512]{1,0:T(2,128)S(1)} %get-tuple-element.502), kind=kOutput, calls=%fused_computation.46.clone.1 | convolution fusion | flops 275908608 | bytes 9179136 | tf_op jit(solution)/shard_map/while/body/eval_jaxpr/hst,thd->shd/dot_general | solution.py:86
  174.1 10.2 %fusion.139 = f32[1024,2,128]{0,2,1:T(8,128)} fusion(bf16[512,2,128]{0,2,1:T(8,128)(2,1)S(1)} %bitcast.135, f32[2,512,1024]{2,1,0:T(8,128)} %fusion.136, f32[1024,2,128]{0,2,1:T(8,128)} %get-tuple-element.559, pred[]{:T(512)S(6)} %compare.3, f32[2,512,1024]{2,1,0:T(8,128)} %get-tuple-element.501, f32[2,512]{1,0:T(2,128)S(1)} %get-tuple-element.502), kind=kOutput, calls=%fused_computation.45.clone.1 | convolution fusion | flops 276301824 | bytes 10752001 | tf_op jit(solution)/shard_map/while/body/eval_jaxpr/hst,shd->thd/dot_general | solution.py:90
  185.3 7.3 %all-to-all-start.5 = ((bf16[8,128,256]{2,1,0:T(8,128)(2,1)}), bf16[8,128,256]{2,1,0:T(8,128)(2,1)S(1)}, u32[]{:S(2)}, u32[]{:S(2)}) async-start(bf16[8,128,256]{2,1,0:T(8,128)(2,1)} %bitcast.143), calls=%async_computation.5 | async-start | bytes 1048576 | tf_op jit(solution)/shard_map/all_to_all | solution.py:123
  192.6 1.3 convert_element_type.101
  194.0 1.1 copy.109
  195.2 11.7 %all-to-all-done.5 = bf16[8,128,256]{2,1,0:T(8,128)(2,1)S(1)} async-done(((bf16[8,128,256]{2,1,0:T(8,128)(2,1)}), bf16[8,128,256]{2,1,0:T(8,128)(2,1)S(1)}, u32[]{:S(2)}, u32[]{:S(2)}) %all-to-all-start.5) | async-done | bytes 524320 | tf_op jit(solution)/shard_map/all_to_all | solution.py:123
  206.8 7.8 %all-to-all-start.6 = ((bf16[8,128,256]{2,1,0:T(8,128)(2,1)}), bf16[8,128,256]{2,1,0:T(8,128)(2,1)}, u32[]{:S(2)}, u32[]{:S(2)}) async-start(bf16[8,128,256]{2,1,0:T(8,128)(2,1)} %copy.109), calls=%async_computation.6 | async-start | bytes 1048576 | tf_op jit(solution)/shard_map/all_to_all | solution.py:124
  214.8 1.1 copy.110
  217.1 11.8 %all-to-all-done.6 = bf16[8,128,256]{2,1,0:T(8,128)(2,1)} async-done(((bf16[8,128,256]{2,1,0:T(8,128)(2,1)}), bf16[8,128,256]{2,1,0:T(8,128)(2,1)}, u32[]{:S(2)}, u32[]{:S(2)}) %all-to-all-start.6) | async-done | bytes 524320 | tf_op jit(solution)/shard_map/all_to_all | solution.py:124
  228.9 7.2 %all-to-all-start.7 = ((bf16[8,128,256]{2,1,0:T(8,128)(2,1)}), bf16[8,128,256]{2,1,0:T(8,128)(2,1)S(1)}, u32[]{:S(2)}, u32[]{:S(2)}) async-start(bf16[8,128,256]{2,1,0:T(8,128)(2,1)} %copy.110), calls=%async_computation.7 | async-start | bytes 1048576 | tf_op jit(solution)/shard_map/all_to_all | solution.py:125
  236.5 1.3 copy.89
  239.8 1.3 copy.98
  243.2 6.7 %all-to-all-done.7 = bf16[8,128,256]{2,1,0:T(8,128)(2,1)S(1)} async-done(((bf16[8,128,256]{2,1,0:T(8,128)(2,1)}), bf16[8,128,256]{2,1,0:T(8,128)(2,1)S(1)}, u32[]{:S(2)}, u32[]{:S(2)}) %all-to-all-start.7) | async-done | bytes 524320 | tf_op jit(solution)/shard_map/all_to_all | solution.py:125
  250.2 1.0 copy.104
  251.2 8.9 %all-reduce.4 = (f32[2048]{0:T(1024)S(1)}, f32[2048]{0:T(1024)S(1)}) all-reduce(f32[2048]{0:T(1024)S(1)} %get-tuple-element.303, f32[2048]{0:T(1024)S(1)} %get-tuple-element.305), channel_id=1, replica_groups=mesh['dp_0'=2,'dp_1'=12,'dp_2'=4,'seq_0'=4,'seq_1'=2] {'dp_0'}, use_global_device_ids=true, to_apply=%region_14.15 | all-reduce | flops 4096 | bytes 32768 | tf_op jit(solution)/shard_map/psum | solution.py:18
  260.2 36.6 %all-reduce = (f32[2048]{0:T(1024)S(1)}, f32[2048]{0:T(1024)S(1)}) all-reduce(f32[2048]{0:T(1024)S(1)} %get-tuple-element.357, f32[2048]{0:T(1024)S(1)} %get-tuple-element.358), channel_id=1, replica_groups=mesh['dp_0'=2,'dp_1'=12,'dp_2'=4,'seq_0'=4,'seq_1'=2] {'dp_1'}, use_global_device_ids=true, to_apply=%region_15.16 | all-reduce | flops 4096 | bytes 32768 | tf_op jit(solution)/shard_map/psum | solution.py:18
  296.7 13.3 %all-reduce.2 = (f32[2048]{0:T(1024)S(1)}, f32[2048]{0:T(1024)S(1)}) all-reduce(f32[2048]{0:T(1024)S(1)} %get-tuple-element.349, f32[2048]{0:T(1024)S(1)} %get-tuple-element.350), channel_id=1, replica_groups=mesh['dp_0'=2,'dp_1'=12,'dp_2'=4,'seq_0'=4,'seq_1'=2] {'dp_2'}, use_global_device_ids=true, to_apply=%region_16.17 | all-reduce | flops 4096 | bytes 32768 | tf_op jit(solution)/shard_map/psum | solution.py:18
  310.0 15.8 %all-reduce.1 = (f32[2048]{0:T(1024)S(1)}, f32[2048]{0:T(1024)S(1)}) all-reduce(f32[2048]{0:T(1024)S(1)} %get-tuple-element.353, f32[2048]{0:T(1024)S(1)} %get-tuple-element.354), channel_id=1, replica_groups=mesh['dp_0'=2,'dp_1'=12,'dp_2'=4,'seq_0'=4,'seq_1'=2] {'seq_0'}, use_global_device_ids=true, to_apply=%region_17.18 | all-reduce | flops 4096 | bytes 32768 | tf_op jit(solution)/shard_map/psum | solution.py:18
  325.8 24.6 %all-reduce.3 = (f32[2048]{0:T(1024)}, f32[2048]{0:T(1024)}) all-reduce(f32[2048]{0:T(1024)S(1)} %get-tuple-element.351, f32[2048]{0:T(1024)S(1)} %get-tuple-element.352), channel_id=1, replica_groups=mesh['dp_0'=2,'dp_1'=12,'dp_2'=4,'seq_0'=4,'seq_1'=2] {'seq_1'}, use_global_device_ids=true, to_apply=%region_18.19 | all-reduce | flops 4096 | bytes 32768 | tf_op jit(solution)/shard_map/psum | solution.py:18
  (94 shorter events, 24.3 us)
Async XLA Ops:
  0.6 17.8 %copy-start.4 = (bf16[128,2048]{1,0:T(8,128)(2,1)S(1)}, bf16[128,2048]{1,0:T(8,128)(2,1)}, u32[]{:S(2)}) copy-start(bf16[128,2048]{1,0:T(8,128)(2,1)} %param.14) | copy-start | bytes 1572868
  0.6 36.7 %copy-start.5 = (bf16[128,2048]{1,0:T(8,128)(2,1)S(1)}, bf16[128,2048]{1,0:T(8,128)(2,1)}, u32[]{:S(2)}) copy-start(bf16[128,2048]{1,0:T(8,128)(2,1)} %param.12) | copy-start | bytes 1572868
  0.7 37.3 %copy-start.7 = (f32[2048]{0:T(1024)S(1)}, f32[2048]{0:T(1024)}, u32[]{:S(2)}) copy-start(f32[2048]{0:T(1024)} %param.15) | copy-start | bytes 24580
  4.4 54.0 %copy-start.9 = (s32[1,1024]{1,0:T(1,128)S(1)}, s32[1,1024]{1,0:T(1,128)}, u32[]{:S(2)}) copy-start(s32[1,1024]{1,0:T(1,128)} %param.19) | copy-start | bytes 12292
  4.4 27.1 %all-to-all-start.1 = ((bf16[128,8,256]{2,0,1:T(8,128)(2,1)}), bf16[128,8,256]{2,0,1:T(8,128)(2,1)S(1)}, u32[]{:S(2)}, u32[]{:S(2)}) async-start(bf16[128,8,256]{2,0,1:T(8,128)(2,1)} %copy.84), calls=%async_computation.1 | async-start | bytes 1048576 | tf_op jit(solution)/shard_map/all_to_all | solution.py:113
  31.5 21.0 %all-to-all-start.2 = ((bf16[128,8,256]{0,2,1:T(8,128)(2,1)}), bf16[128,8,256]{0,2,1:T(8,128)(2,1)S(1)}, u32[]{:S(2)}, u32[]{:S(2)}) async-start(bf16[128,8,256]{0,2,1:T(8,128)(2,1)} %bitcast.5), calls=%async_computation.2 | async-start | bytes 1048576 | tf_op jit(solution)/shard_map/all_to_all | solution.py:114
  52.5 18.0 %all-to-all-start = ((bf16[128,8,256]{0,2,1:T(8,128)(2,1)}), bf16[128,8,256]{0,2,1:T(8,128)(2,1)S(1)}, u32[]{:S(2)}, u32[]{:S(2)}) async-start(bf16[128,8,256]{0,2,1:T(8,128)(2,1)} %bitcast.1), calls=%async_computation | async-start | bytes 1048576 | tf_op jit(solution)/shard_map/all_to_all | solution.py:112
  56.3 22.4 %copy-start.3 = (s32[1,1024]{1,0:T(1,128)S(1)}, s32[1,1024]{1,0:T(1,128)}, u32[]{:S(2)}) copy-start(s32[1,1024]{1,0:T(1,128)} %param.18) | copy-start | bytes 12292
  70.5 32.3 %all-to-all-start.4 = ((bf16[128,8,256]{0,2,1:T(8,128)(2,1)}), bf16[128,8,256]{0,2,1:T(8,128)(2,1)S(1)}, u32[]{:S(2)}, u32[]{:S(2)}) async-start(bf16[128,8,256]{0,2,1:T(8,128)(2,1)} %bitcast.10), calls=%async_computation.4 | async-start | bytes 1048576 | tf_op jit(solution)/shard_map/all_to_all | solution.py:118
  102.8 82.5 %all-to-all-start.3 = ((bf16[8,128,256]{2,1,0:T(8,128)(2,1)}), bf16[8,128,256]{2,1,0:T(8,128)(2,1)}, u32[]{:S(2)}, u32[]{:S(2)}) async-start(bf16[8,128,256]{2,1,0:T(8,128)(2,1)} %bitcast.144), calls=%async_computation.3 | async-start | bytes 1048576 | tf_op jit(solution)/shard_map/all_to_all | solution.py:117
  123.4 2.7 copy-start.6
  137.3 10.1 %copy-start = (bf16[2,512,256]{2,1,0:T(8,128)(2,1)S(1)}, bf16[2,512,256]{2,1,0:T(8,128)(2,1)}, u32[]{:S(2)}) copy-start(bf16[2,512,256]{2,1,0:T(8,128)(2,1)} %get-tuple-element.561) | copy-start | bytes 1572868 | tf_op jit(solution)/shard_map/while
  147.5 0.8 copy-start.1
  160.2 2.7 copy-start.6
  174.1 10.4 %copy-start = (bf16[2,512,256]{2,1,0:T(8,128)(2,1)S(1)}, bf16[2,512,256]{2,1,0:T(8,128)(2,1)}, u32[]{:S(2)}) copy-start(bf16[2,512,256]{2,1,0:T(8,128)(2,1)} %get-tuple-element.561) | copy-start | bytes 1572868 | tf_op jit(solution)/shard_map/while
  184.5 0.8 copy-start.1
  185.3 29.4 %copy-start.2 = (f32[1024,2,128]{0,2,1:T(8,128)S(1)}, f32[1024,2,128]{0,2,1:T(8,128)}, u32[]{:S(2)}) copy-start(f32[1024,2,128]{0,2,1:T(8,128)} %get-tuple-element.130) | copy-start | bytes 3145732
  185.3 21.5 %all-to-all-start.5 = ((bf16[8,128,256]{2,1,0:T(8,128)(2,1)}), bf16[8,128,256]{2,1,0:T(8,128)(2,1)S(1)}, u32[]{:S(2)}, u32[]{:S(2)}) async-start(bf16[8,128,256]{2,1,0:T(8,128)(2,1)} %bitcast.143), calls=%async_computation.5 | async-start | bytes 1048576 | tf_op jit(solution)/shard_map/all_to_all | solution.py:123
  206.8 22.1 %all-to-all-start.6 = ((bf16[8,128,256]{2,1,0:T(8,128)(2,1)}), bf16[8,128,256]{2,1,0:T(8,128)(2,1)}, u32[]{:S(2)}, u32[]{:S(2)}) async-start(bf16[8,128,256]{2,1,0:T(8,128)(2,1)} %copy.109), calls=%async_computation.6 | async-start | bytes 1048576 | tf_op jit(solution)/shard_map/all_to_all | solution.py:124
  216.4 24.7 %copy-start.8 = (f32[2048]{0:T(1024)S(1)}, f32[2048]{0:T(1024)}, u32[]{:S(2)}) copy-start(f32[2048]{0:T(1024)} %param.16) | copy-start | bytes 24580
  228.9 21.0 %all-to-all-start.7 = ((bf16[8,128,256]{2,1,0:T(8,128)(2,1)}), bf16[8,128,256]{2,1,0:T(8,128)(2,1)S(1)}, u32[]{:S(2)}, u32[]{:S(2)}) async-start(bf16[8,128,256]{2,1,0:T(8,128)(2,1)} %copy.110), calls=%async_computation.7 | async-start | bytes 1048576 | tf_op jit(solution)/shard_map/all_to_all | solution.py:125
where the time goes:
time: 352 us; the launch traced here: 350 us
  blocking collectives  99.2 us (28%)
  matrix products  81 us (23%)
  waiting for transfers between devices  65.3 us (19%)
  starting transfers between devices  60.7 us (17%)
  local copies, waits for them, and re-layouts  31.5 us (9%)
  other arithmetic  8.97 us (3%)
    psum x5, blocking collectives, by_axis(): value = lax.psum(value, axis)  99.2 us
    dot_general x2, matrix products, one_block(): jnp.einsum('hst,thd->shd', score_grad, k_three, preferred_element_type=jn...  22.4 us
    dot_general x2, matrix products, one_block(): jnp.einsum('hst,shd->thd', score_grad, q_block, preferred_element_type=jn...  20.2 us
    sub x4, matrix products, one_block(): weights = jnp.exp(scores - row_max)  18.8 us
    all_to_all x1, starting transfers between devices, per_device(): lax.all_to_all(k_norm, SEQ, split_axis=1, concat_axis=0, tiled=True)  14 us
    all_to_all x1, waiting for transfers between devices, per_device(): lax.all_to_all(values, SEQ, split_axis=1, concat_axis=0, tiled=True)  13.4 us
    unnamed x27, local copies, waits for them, and re-layouts  12.2 us
    all_to_all x1, waiting for transfers between devices, per_device(): lax.all_to_all(k_norm, SEQ, split_axis=1, concat_axis=0, tiled=True)  12.1 us
  transfers between devices with their start and end apart: 8, of which 6 were waited for; matrix products, arithmetic and copies ran while one was open for 33% of the time, Pallas kernels for 0%

commit v1 on v0

v1 whole, which is shorter than its diff:
```python
import functools

import jax
import jax.numpy as jnp
from jax import lax
from jax.experimental import pallas as pl
from jax.experimental.pallas import tpu as pltpu
from jax.sharding import Mesh
from jax.sharding import PartitionSpec as P

D_HEAD = 128
DP_SEQ = ("dp_0", "dp_1", "dp_2", "seq_0", "seq_1")
DP = ("dp_0", "dp_1", "dp_2")
MESH = pl.DeviceIdType.MESH

epsilon = 1e-06
N_SEQ = 8
ROWS = 128
LEN = 1024
WIDTH = 2048
BLOCK = 256
SCALE = D_HEAD ** (-0.5)
LOG2E = 1.4426950408889634
SLOTS = 16


def nt(a, b):
    return lax.dot_general(a, b, (((1,), (1,)), ((), ())), preferred_element_type=jnp.float32)


def tn(a, b):
    return lax.dot_general(a, b, (((0,), (0,)), ((), ())), preferred_element_type=jnp.float32)


def nn(a, b):
    return lax.dot_general(a, b, (((1,), (0,)), ((), ())), preferred_element_type=jnp.float32)


def wide(gain_ref):
    return jnp.concatenate([gain_ref[r : r + 1, :] for r in range(WIDTH // 128)], axis=1)


def kernel(
    q_ref, k_ref, v_ref, g_ref, qg_ref, kg_ref, seg_ref, vis_ref,
    o_ref, dq_ref, dk_ref, dv_ref, gq_ref, gk_ref,
    qn, kn, qi, ki, rx, tx, rdq, rdk, code, acc_k, acc_v, part, gx, gz, gy,
    in_send, in_recv, out_send, out_recv, g_send, g_recv,
):
    ylo, z, x = lax.axis_index("dp_0"), lax.axis_index("dp_1"), lax.axis_index("dp_2")
    chip, core = lax.axis_index("seq_0"), lax.axis_index("seq_1")
    me = chip * 2 + core

    barrier = pltpu.get_barrier_semaphore()

    def greet(device):
        pl.semaphore_signal(barrier, inc=1, device_id=device, device_id_type=MESH)

    def member(step):
        other = lax.rem(me + step, N_SEQ)
        return other, {"seq_0": other // 2, "seq_1": lax.rem(other, 2)}

    def across(step):
        other = lax.rem(ylo * N_SEQ + me + step, SLOTS)
        return {
            "dp_0": other // N_SEQ,
            "seq_0": lax.rem(other, N_SEQ) // 2,
            "seq_1": lax.rem(other, 2),
        }

    x_peers = [{"dp_2": lax.rem(x + d, 4)} for d in range(1, 4)]
    z_peers = [{"dp_1": lax.rem(z + d, 12)} for d in range(1, 12)]
    y_peers = [across(d) for d in range(1, SLOTS)]
    everyone = y_peers + x_peers + z_peers
    for device in everyone:
        greet(device)

    def normalize(raw_ref, gain, out, inv_ref):
        def rows_of(i, _):
            rows = pl.ds(pl.multiple_of(i * 16, 16), 16)
            raw = raw_ref[rows, :].astype(jnp.float32)
            inv = lax.rsqrt(jnp.mean(raw * raw, axis=-1, keepdims=True) + epsilon)
            inv_ref[rows, :] = jnp.broadcast_to(inv, (16, 128))
            out[rows, :] = (raw * inv * gain).astype(jnp.bfloat16)
            return 0

        lax.fori_loop(0, ROWS // 16, rows_of, 0)

    part[...] = jnp.zeros_like(part)
    q_gain, k_gain = wide(qg_ref), wide(kg_ref)
    normalize(q_ref, q_gain, qn, qi)
    normalize(k_ref, k_gain, kn, ki)
    sources = (qn, kn, v_ref, g_ref)
    my_rows = pl.ds(pl.multiple_of(me * ROWS, ROWS), ROWS)

    def columns(device, h):
        return pl.ds(pl.multiple_of(device * 256 + h * 128, 128), 128)

    pl.semaphore_wait(barrier, len(everyone))

    for h in range(2):
        for a in range(4):
            for step in (2, 3, 6, 7, 4, 5, 1):
                other, device = member(step)
                pltpu.make_async_remote_copy(
                    src_ref=sources[a].at[:, columns(other, h)],
                    dst_ref=rx.at[a, h, my_rows],
                    send_sem=in_send.at[a, h],
                    recv_sem=in_recv.at[a, h],
                    device_id=device,
                    device_id_type=MESH,
                ).start()
    for h in range(2):
        for a in range(4):
            rx[a, h, my_rows, :] = sources[a][:, columns(me, h)]

    seg_row = seg_ref[...].astype(jnp.float32)
    key_row = jnp.where(vis_ref[...] == 1, seg_row, -1.0)
    for j in range(LEN // 128):
        piece = jnp.broadcast_to(key_row[:, j * 128 : (j + 1) * 128], (128, 128))
        code[j * 128 : (j + 1) * 128, :] = piece.T

    def of_all(a, h, sends, recvs):
        return pltpu.make_async_remote_copy(
            src_ref=rx.at[a, h, pl.ds(0, 7 * ROWS)],
            dst_ref=rx.at[a, h, pl.ds(0, 7 * ROWS)],
            send_sem=sends.at[a, h],
            recv_sem=recvs.at[a, h],
            device_id=member(1)[1],
            device_id_type=MESH,
        )

    landing = (o_ref, rdq, rdk, dv_ref)

    def send_out(a, h, other):
        pltpu.make_async_remote_copy(
            src_ref=tx.at[a, h, pl.ds(pl.multiple_of(other * ROWS, ROWS), ROWS)],
            dst_ref=landing[a].at[:, columns(me, h)],
            send_sem=out_send.at[a, h],
            recv_sem=out_recv.at[a, h],
            device_id={"seq_0": other // 2, "seq_1": lax.rem(other, 2)},
            device_id_type=MESH,
        ).start()

    def keep_own(a, h):
        landing[a][:, columns(me, h)] = tx[a, h, my_rows, :]

    for h in range(2):
        for a in range(4):
            of_all(a, h, in_send, in_recv).wait_recv()
        acc_k[...] = jnp.zeros_like(acc_k)
        acc_v[...] = jnp.zeros_like(acc_v)

        def block(t, gain_sum):
            at_chip = lax.rem(chip + 1 + t, 4)
            start = pl.multiple_of(at_chip * BLOCK, BLOCK)
            rows = pl.ds(start, BLOCK)
            q_i, g_i = rx[0, h, rows, :], rx[3, h, rows, :]
            keys, vals = rx[1, h], rx[2, h]
            seg_i = seg_ref[:, rows].astype(jnp.float32)
            k_code = code[...]
            k_code = jnp.concatenate([k_code, k_code], axis=1)
            key_at = lax.broadcasted_iota(jnp.int32, (LEN, BLOCK), 0)
            query_at = lax.broadcasted_iota(jnp.int32, (LEN, BLOCK), 1) + start
            allowed = (k_code == seg_i) | (key_at == query_at)
            scores = jnp.where(allowed, nt(keys, q_i), -1e30)
            top = jnp.max(scores, axis=0, keepdims=True)
            weights = jnp.exp2((scores - top) * (SCALE * LOG2E))
            prob = weights * (1.0 / jnp.sum(weights, axis=0, keepdims=True))
            half = prob.astype(jnp.bfloat16)
            tx[0, h, rows, :] = tn(vals, half).T.astype(jnp.bfloat16)
            dprob = nt(vals, g_i)
            dot = jnp.sum(prob * dprob, axis=0, keepdims=True)
            grad = (prob * (dprob - dot) * SCALE).astype(jnp.bfloat16)
            dq_i = tn(keys, grad).T.astype(jnp.bfloat16)
            tx[1, h, rows, :] = dq_i
            acc_v[...] += nn(half, g_i)
            acc_k[...] += nn(grad, q_i)
            for c in range(2):
                other = at_chip * 2 + c

                @pl.when(other != me)
                def _():
                    send_out(0, h, other)
                    send_out(1, h, other)

            return gain_sum + jnp.sum(
                dq_i.astype(jnp.float32) * q_i.astype(jnp.float32), axis=0, keepdims=True
            )

        q_sum = lax.fori_loop(0, LEN // BLOCK, block, jnp.zeros((1, D_HEAD), jnp.float32))
        tx[2, h] = acc_k[...].astype(jnp.bfloat16)
        tx[3, h] = acc_v[...].astype(jnp.bfloat16)
        for a in (2, 3):
            for step in (2, 3, 6, 7, 4, 5, 1):
                send_out(a, h, member(step)[0])
        for a in range(4):
            keep_own(a, h)
        k_sum = jnp.sum(
            tx[2, h].astype(jnp.float32) * rx[1, h].astype(jnp.float32), axis=0, keepdims=True
        )
        part[h : h + 1, :] = q_sum / qg_ref[pl.ds(me * 2 + h, 1), :]
        part[2 + h : 3 + h, :] = k_sum / kg_ref[pl.ds(me * 2 + h, 1), :]

    def spread(slot, peers, sem):
        copies = []
        for device in peers:
            pltpu.make_async_remote_copy(
                src_ref=slot, dst_ref=slot, send_sem=g_send.at[sem], recv_sem=g_recv.at[sem],
                device_id=device, device_id_type=MESH,
            ).start()

    def settle(slots, peers, sem):
        copy = pltpu.make_async_remote_copy(
            src_ref=slots.at[pl.ds(0, len(peers))], dst_ref=slots.at[pl.ds(0, len(peers))],
            send_sem=g_send.at[sem], recv_sem=g_recv.at[sem],
            device_id=peers[0], device_id_type=MESH,
        )
        copy.wait_recv()
        copy.wait_send()

    gx[x] = part[...]
    spread(gx.at[x], x_peers, 0)
    settle(gx, x_peers, 0)
    gz[z] = (gx[0] + gx[1]) + (gx[2] + gx[3])
    spread(gz.at[z], z_peers, 1)
    settle(gz, z_peers, 1)
    total = gz[0]
    for i in range(1, 12):
        total = total + gz[i]
    slot = ylo * N_SEQ + me
    gy[slot] = total
    spread(gy.at[slot], y_peers, 2)

    def norm_back(raw_ref, inv_ref, gain, grads, out):
        def rows_of(i, _):
            rows = pl.ds(pl.multiple_of(i * 16, 16), 16)
            raw = raw_ref[rows, :].astype(jnp.float32)
            inv = inv_ref[rows, :][:, 0:1]
            scaled = gain * grads[rows, :].astype(jnp.float32)
            mean_term = jnp.mean(scaled * raw, axis=-1, keepdims=True)
            out[rows, :] = (inv * scaled - raw * (inv * inv * inv * mean_term)).astype(jnp.bfloat16)
            return 0

        lax.fori_loop(0, ROWS // 16, rows_of, 0)

    for h in range(2):
        of_all(1, h, out_send, out_recv).wait_recv()
    norm_back(q_ref, qi, q_gain, rdq, dq_ref)
    for h in range(2):
        of_all(2, h, out_send, out_recv).wait_recv()
    norm_back(k_ref, ki, k_gain, rdk, dk_ref)
    for a in (0, 3):
        for h in range(2):
            of_all(a, h, out_send, out_recv).wait_recv()
    settle(gy, y_peers, 2)
    for s in range(N_SEQ):
        both = gy[s] + gy[N_SEQ + s]
        gq_ref[2 * s : 2 * s + 2, :] = both[0:2, :]
        gk_ref[2 * s : 2 * s + 2, :] = both[2:4, :]
    for h in range(2):
        for a in range(4):
            of_all(a, h, in_send, in_recv).wait_send()
            of_all(a, h, out_send, out_recv).wait_send()


def per_device(queries, keys, values, q_gain, k_gain, out_grad, segments, visible):
    vmem = pl.BlockSpec(memory_space=pltpu.VMEM)
    rows = jax.ShapeDtypeStruct((ROWS, WIDTH), jnp.bfloat16)
    gains = jax.ShapeDtypeStruct((WIDTH // 128, 128), jnp.float32)
    dma = pltpu.SemaphoreType.DMA
    bf16, f32 = jnp.bfloat16, jnp.float32
    attn_out, query_grad, key_grad, value_grad, gq, gk = pl.pallas_call(
        kernel,
        out_shape=(rows, rows, rows, rows, gains, gains),
        in_specs=[vmem] * 8,
        out_specs=[vmem] * 6,
        scratch_shapes=[
            pltpu.VMEM((ROWS, WIDTH), bf16),
            pltpu.VMEM((ROWS, WIDTH), bf16),
            pltpu.VMEM((ROWS, 128), f32),
            pltpu.VMEM((ROWS, 128), f32),
            pltpu.VMEM((4, 2, LEN, D_HEAD), bf16),
            pltpu.VMEM((4, 2, LEN, D_HEAD), bf16),
            pltpu.VMEM((ROWS, WIDTH), bf16),
            pltpu.VMEM((ROWS, WIDTH), bf16),
            pltpu.VMEM((LEN, 128), f32),
            pltpu.VMEM((LEN, D_HEAD), f32),
            pltpu.VMEM((LEN, D_HEAD), f32),
            pltpu.VMEM((8, 128), f32),
            pltpu.VMEM((4, 8, 128), f32),
            pltpu.VMEM((12, 8, 128), f32),
            pltpu.VMEM((SLOTS, 8, 128), f32),
            dma((4, 2)), dma((4, 2)), dma((4, 2)), dma((4, 2)), dma((3,)), dma((3,)),
        ],
        compiler_params=pltpu.CompilerParams(
            collective_id=0, has_side_effects=True, vmem_limit_bytes=48 * 2**20
        ),
        name="packed_attention",
    )(
        queries, keys, values, out_grad,
        q_gain.reshape(WIDTH // 128, 128), k_gain.reshape(WIDTH // 128, 128),
        segments, visible,
    )
    return (attn_out, query_grad, key_grad, value_grad, gq.reshape(WIDTH), gk.reshape(WIDTH))


def solution(mesh):
    finer = Mesh(mesh.devices.reshape(2, 12, 4, 4, 2), ("dp_0", "dp_1", "dp_2", "seq_0", "seq_1"))
    placed = (
        P(DP_SEQ, None),
        P(DP_SEQ, None),
        P(DP_SEQ, None),
        P(),
        P(),
        P(DP_SEQ, None),
        P(DP, None),
        P(DP, None),
    )
    return jax.shard_map(
        per_device,
        mesh=finer,
        in_specs=placed,
        out_specs=(P(DP_SEQ, None), P(DP_SEQ, None), P(DP_SEQ, None), P(DP_SEQ, None), P(), P()),
        check_vma=False,
    )
```

time: 352 us -> 135 us (0.38)
  Pallas kernels: 0 us -> 123 us
  blocking collectives: 99.2 us -> 0 us
  matrix products: 81 us -> 0 us
  waiting for transfers between devices: 65.3 us -> 0 us
  starting transfers between devices: 60.7 us -> 0 us
  local copies, waits for them, and re-layouts: 31.5 us -> 11.3 us
  other arithmetic: 8.97 us -> 0 us
    pallas_call x0 -> x1, Pallas kernels: none -> 123 us  [per_device(): pl.pallas_call(kernel, out_shape=(rows, rows, rows, rows, gains, gains),...]
    psum x5 -> x0, blocking collectives: 99.2 us -> none  [by_axis(): value = lax.psum(value, axis)]
    all_to_all x8 -> x0, waiting for transfers between devices: 65.3 us -> none  [the longest x1 13.4 us: per_device(): lax.all_to_all(values, SEQ, split_axis=1, concat_axis=0, tiled=True)]
    dot_general x10 -> x0, matrix products: 62.2 us -> none  [the longest x2 22.4 us: one_block(): jnp.einsum('hst,thd->shd', score_grad, k_three, preferred_element_type=jn...]
    all_to_all x8 -> x0, starting transfers between devices: 60.7 us -> none  [the longest x1 14 us: per_device(): lax.all_to_all(k_norm, SEQ, split_axis=1, concat_axis=0, tiled=True)]
    sub x4 -> x0, matrix products: 18.8 us -> none  [one_block(): weights = jnp.exp(scores - row_max)]
    all_to_all x7 -> x0, local copies, waits for them, and re-layouts: 5.33 us -> none  [the longest x1 1.31 us: per_device(): lax.all_to_all(out_part, SEQ, split_axis=0, concat_axis=1, tiled=True)]
    dynamic_slice x16 -> x0, local copies, waits for them, and re-layouts: 4.95 us -> none  [the longest x4 2.33 us: attend(): lax.scan(one_block, (empty, empty), jnp.arange(block_count, dtype=jnp.int...]
  transfers between devices with their start and end apart: 8 -> 0, of which waited for: 6 -> 0; matrix products, arithmetic and copies ran while one was open for 33% -> 0% of each run, Pallas kernels for 0% -> 0%
where the time goes in v1:
time: 135 us
  Pallas kernels  123 us (91%)
  local copies, waits for them, and re-layouts  11.3 us (8%)
    pallas_call x1, Pallas kernels, per_device(): pl.pallas_call(kernel, out_shape=(rows, rows, rows, rows, gains, gains),...  123 us
    unnamed x22, local copies, waits for them, and re-layouts  11.3 us

profile of v1, /device:TPU:1, one launch (start us, length us, event | category | flops | bytes accessed | tf_op | source)
XLA Modules:
  0.0 134.7 jit_solution(15032240814117958449)
XLA Ops:
  0.6 0.0 copy-start
  0.6 1.0 copy-done
  1.7 0.0 copy-start.1
  1.7 1.0 copy-done.1
  2.7 0.0 copy-start.2
  2.7 1.0 copy-done.2
  3.8 0.0 copy-start.3
  3.8 1.0 copy-done.3
  4.8 0.0 copy-start.4
  4.8 0.7 copy-done.4
  5.5 0.0 copy-start.5
  5.5 0.7 copy-done.5
  6.2 0.0 copy-start.6
  6.2 0.7 copy-done.6
  6.9 0.0 copy-start.7
  6.9 0.7 copy-done.7
  7.6 122.7 %packed_attention.1 = (bf16[128,2048]{1,0:T(8,128)(2,1)S(1)}, bf16[128,2048]{1,0:T(8,128)(2,1)S(1)}, bf16[128,2048]{1,0:T(8,128)(2,1)S(1)}, bf16[128,2048]{1,0:T...) custom-call(bf16[128,2048]{1,0:T(8,128)(2,1)S(1)} %copy-done, bf16[128,2048]{1,0:T(8,128)(2,1)S(1)} %copy-done.1, ...), custom_call_target="tpu_custom_call" | custom-call | tf_op jit(solution)/shard_map/packed_attention/pallas_call | solution.py:272
  130.3 0.8 copy.20
  131.1 0.8 copy.21
  131.9 0.8 copy.22
  132.7 0.8 copy.23
  133.5 0.6 copy.24
  134.1 0.6 copy.25
Async XLA Ops:
  0.6 1.0 copy-start
  1.7 1.0 copy-start.1
  2.7 1.0 copy-start.2
  3.8 1.0 copy-start.3
  4.8 0.7 copy-start.4
  5.5 0.7 copy-start.5
  6.2 0.7 copy-start.6
  6.9 0.7 copy-start.7

commit v2 on v1

--- a/solution.py
+++ b/solution.py
@@ -41,16 +41,30 @@
 
 
 def kernel(
+    q_hbm, k_hbm, v_hbm, g_hbm, qg_hbm, kg_hbm, seg_hbm, vis_hbm,
+    o_ref, dq_ref, dk_ref, dv_ref, gq_ref, gk_ref,
     q_ref, k_ref, v_ref, g_ref, qg_ref, kg_ref, seg_ref, vis_ref,
-    o_ref, dq_ref, dk_ref, dv_ref, gq_ref, gk_ref,
     qn, kn, qi, ki, rx, tx, rdq, rdk, code, acc_k, acc_v, part, gx, gz, gy,
-    in_send, in_recv, out_send, out_recv, g_send, g_recv,
+    in_send, in_recv, out_send, out_recv, g_send, g_recv, load_sem, ready, line, go,
 ):
     ylo, z, x = lax.axis_index("dp_0"), lax.axis_index("dp_1"), lax.axis_index("dp_2")
     chip, core = lax.axis_index("seq_0"), lax.axis_index("seq_1")
     me = chip * 2 + core
 
+    loads = [
+        pltpu.make_async_copy(source, target, load_sem.at[i])
+        for i, (source, target) in enumerate(
+            (
+                (qg_hbm, qg_ref), (q_hbm, q_ref), (kg_hbm, kg_ref), (k_hbm, k_ref),
+                (v_hbm, v_ref), (g_hbm, g_ref), (seg_hbm, seg_ref), (vis_hbm, vis_ref),
+            )
+        )
+    ]
+    for load in loads:
+        load.start()
+
     barrier = pltpu.get_barrier_semaphore()
+    leader = me == 0
 
     def greet(device):
         pl.semaphore_signal(barrier, inc=1, device_id=device, device_id_type=MESH)
@@ -70,9 +84,18 @@
     x_peers = [{"dp_2": lax.rem(x + d, 4)} for d in range(1, 4)]
     z_peers = [{"dp_1": lax.rem(z + d, 12)} for d in range(1, 12)]
     y_peers = [across(d) for d in range(1, SLOTS)]
-    everyone = y_peers + x_peers + z_peers
-    for device in everyone:
-        greet(device)
+    leaders = x_peers + z_peers + [{"dp_0": 1 - ylo}]
+    for step in range(1, N_SEQ):
+        other, device = member(step)
+
+        @pl.when(other != 0)
+        def _():
+            greet(device)
+
+    @pl.when(leader)
+    def _():
+        for device in leaders:
+            greet(device)
 
     def normalize(raw_ref, gain, out, inv_ref):
         def rows_of(i, _):
@@ -86,16 +109,32 @@
         lax.fori_loop(0, ROWS // 16, rows_of, 0)
 
     part[...] = jnp.zeros_like(part)
-    q_gain, k_gain = wide(qg_ref), wide(kg_ref)
+    loads[0].wait()
+    loads[1].wait()
+    q_gain = wide(qg_ref)
     normalize(q_ref, q_gain, qn, qi)
+    loads[2].wait()
+    loads[3].wait()
+    k_gain = wide(kg_ref)
     normalize(k_ref, k_gain, kn, ki)
+    for load in loads[4:]:
+        load.wait()
     sources = (qn, kn, v_ref, g_ref)
     my_rows = pl.ds(pl.multiple_of(me * ROWS, ROWS), ROWS)
 
     def columns(device, h):
         return pl.ds(pl.multiple_of(device * 256 + h * 128, 128), 128)
 
-    pl.semaphore_wait(barrier, len(everyone))
+    @pl.when(me != 0)
+    def _():
+        pl.semaphore_wait(barrier, N_SEQ - 1)
+        pl.semaphore_signal(
+            ready, inc=1, device_id={"seq_0": 0, "seq_1": 0}, device_id_type=MESH
+        )
+
+    @pl.when(leader)
+    def _():
+        pl.semaphore_wait(ready, N_SEQ - 1)
 
     for h in range(2):
         for a in range(4):
@@ -141,12 +180,19 @@
             device_id_type=MESH,
         ).start()
 
+    def send_all(a, h):
+        for step in (2, 3, 6, 7, 4, 5, 1):
+            send_out(a, h, member(step)[0])
+
     def keep_own(a, h):
         landing[a][:, columns(me, h)] = tx[a, h, my_rows, :]
 
     for h in range(2):
         for a in range(4):
             of_all(a, h, in_send, in_recv).wait_recv()
+        if h == 1:
+            for a in range(4):
+                send_all(a, 0)
         acc_k[...] = jnp.zeros_like(acc_k)
         acc_v[...] = jnp.zeros_like(acc_v)
 
@@ -175,13 +221,14 @@
             tx[1, h, rows, :] = dq_i
             acc_v[...] += nn(half, g_i)
             acc_k[...] += nn(grad, q_i)
-            for c in range(2):
-                other = at_chip * 2 + c
-
-                @pl.when(other != me)
-                def _():
-                    send_out(0, h, other)
-                    send_out(1, h, other)
+            if h == 1:
+                for c in range(2):
+                    other = at_chip * 2 + c
+
+                    @pl.when(other != me)
+                    def _():
+                        send_out(0, h, other)
+                        send_out(1, h, other)
 
             return gain_sum + jnp.sum(
                 dq_i.astype(jnp.float32) * q_i.astype(jnp.float32), axis=0, keepdims=True
@@ -190,14 +237,22 @@
         q_sum = lax.fori_loop(0, LEN // BLOCK, block, jnp.zeros((1, D_HEAD), jnp.float32))
         tx[2, h] = acc_k[...].astype(jnp.bfloat16)
         tx[3, h] = acc_v[...].astype(jnp.bfloat16)
-        for a in (2, 3):
-            for step in (2, 3, 6, 7, 4, 5, 1):
-                send_out(a, h, member(step)[0])
+        if h == 1:
+            for a in (2, 3):
+                send_all(a, h)
         for a in range(4):
             keep_own(a, h)
         k_sum = jnp.sum(
             tx[2, h].astype(jnp.float32) * rx[1, h].astype(jnp.float32), axis=0, keepdims=True
         )
+        if h == 0:
+
+            @pl.when(leader)
+            def _():
+                pl.semaphore_wait(barrier, len(leaders))
+                for device in leaders:
+                    pl.semaphore_signal(line, inc=1, device_id=device, device_id_type=MESH)
+
         part[h : h + 1, :] = q_sum / qg_ref[pl.ds(me * 2 + h, 1), :]
         part[2 + h : 3 + h, :] = k_sum / kg_ref[pl.ds(me * 2 + h, 1), :]
 
@@ -217,6 +272,16 @@
         )
         copy.wait_recv()
         copy.wait_send()
+
+    @pl.when(leader)
+    def _():
+        pl.semaphore_wait(line, len(leaders))
+        for step in range(1, N_SEQ):
+            pl.semaphore_signal(go, inc=1, device_id=member(step)[1], device_id_type=MESH)
+
+    @pl.when(me != 0)
+    def _():
+        pl.semaphore_wait(go, 1)
 
     gx[x] = part[...]
     spread(gx.at[x], x_peers, 0)
@@ -263,18 +328,38 @@
             of_all(a, h, out_send, out_recv).wait_send()
 
 
+def store(*refs):
+    n = 6
+    sources, targets, sem = refs[:n], refs[n : 2 * n], refs[2 * n]
+    copies = [pltpu.make_async_copy(sources[i], targets[i], sem.at[i]) for i in range(n)]
+    for copy in copies:
+        copy.start()
+    for copy in copies:
+        copy.wait()
+
+
 def per_device(queries, keys, values, q_gain, k_gain, out_grad, segments, visible):
     vmem = pl.BlockSpec(memory_space=pltpu.VMEM)
     rows = jax.ShapeDtypeStruct((ROWS, WIDTH), jnp.bfloat16)
     gains = jax.ShapeDtypeStruct((WIDTH // 128, 128), jnp.float32)
     dma = pltpu.SemaphoreType.DMA
     bf16, f32 = jnp.bfloat16, jnp.float32
-    attn_out, query_grad, key_grad, value_grad, gq, gk = pl.pallas_call(
+    hbm = pl.BlockSpec(memory_space=pltpu.HBM)
+    outs = (rows, rows, rows, rows, gains, gains)
+    made = pl.pallas_call(
         kernel,
-        out_shape=(rows, rows, rows, rows, gains, gains),
-        in_specs=[vmem] * 8,
+        out_shape=outs,
+        in_specs=[hbm] * 8,
         out_specs=[vmem] * 6,
         scratch_shapes=[
+            pltpu.VMEM((ROWS, WIDTH), bf16),
+            pltpu.VMEM((ROWS, WIDTH), bf16),
+            pltpu.VMEM((ROWS, WIDTH), bf16),
+            pltpu.VMEM((ROWS, WIDTH), bf16),
+            pltpu.VMEM((WIDTH // 128, 128), f32),
+            pltpu.VMEM((WIDTH // 128, 128), f32),
+            pltpu.VMEM((1, LEN), jnp.int32),
+            pltpu.VMEM((1, LEN), jnp.int32),
             pltpu.VMEM((ROWS, WIDTH), bf16),
             pltpu.VMEM((ROWS, WIDTH), bf16),
             pltpu.VMEM((ROWS, 128), f32),
@@ -290,17 +375,32 @@
             pltpu.VMEM((4, 8, 128), f32),
             pltpu.VMEM((12, 8, 128), f32),
             pltpu.VMEM((SLOTS, 8, 128), f32),
-            dma((4, 2)), dma((4, 2)), dma((4, 2)), dma((4, 2)), dma((3,)), dma((3,)),
+            dma((4, 2)), dma((4, 2)), dma((4, 2)), dma((4, 2)), dma((3,)), dma((3,)), dma((8,)),
+            pltpu.SemaphoreType.REGULAR, pltpu.SemaphoreType.REGULAR, pltpu.SemaphoreType.REGULAR,
         ],
         compiler_params=pltpu.CompilerParams(
             collective_id=0, has_side_effects=True, vmem_limit_bytes=48 * 2**20
         ),
         name="packed_attention",
     )(
-        queries, keys, values, out_grad,
-        q_gain.reshape(WIDTH // 128, 128), k_gain.reshape(WIDTH // 128, 128),
-        segments, visible,
+        *[
+            pltpu.with_memory_space_constraint(array, pltpu.HBM)
+            for array in (
+                queries, keys, values, out_grad,
+                q_gain.reshape(WIDTH // 128, 128), k_gain.reshape(WIDTH // 128, 128),
+                segments, visible,
+            )
+        ]
     )
+    attn_out, query_grad, key_grad, value_grad, gq, gk = pl.pallas_call(
+        store,
+        out_shape=outs,
+        in_specs=[vmem] * 6,
+        out_specs=[hbm] * 6,
+        scratch_shapes=[dma((6,))],
+        compiler_params=pltpu.CompilerParams(vmem_limit_bytes=16 * 2**20),
+        name="store",
+    )(*made)
     return (attn_out, query_grad, key_grad, value_grad, gq.reshape(WIDTH), gk.reshape(WIDTH))
 
 

time: 135 us -> 108 us (0.80)
  Pallas kernels: 123 us -> 106 us
  local copies, waits for them, and re-layouts: 11.3 us -> 0 us
    pallas_call x1 -> x2, Pallas kernels: 123 us -> 106 us  [the longest x1 105 us: per_device(): pl.pallas_call(kernel, out_shape=outs, in_specs=[hbm] * 8, out_specs=[vme...]
    unnamed x22 -> x0, local copies, waits for them, and re-layouts: 11.3 us -> none
where the time goes in v2:
time: 108 us; the launch traced here: 107 us
  Pallas kernels  106 us (98%)
    pallas_call x1, Pallas kernels, per_device(): pl.pallas_call(kernel, out_shape=outs, in_specs=[hbm] * 8, out_specs=[vme...  105 us

profile of v2, /device:TPU:1, one launch (start us, length us, event | category | flops | bytes accessed | tf_op | source)
XLA Modules:
  0.0 106.8 jit_solution(14209811009334955697)
XLA Ops:
  0.6 104.8 %packed_attention.1 = (bf16[128,2048]{1,0:T(8,128)(2,1)S(1)}, bf16[128,2048]{1,0:T(8,128)(2,1)S(1)}, bf16[128,2048]{1,0:T(8,128)(2,1)S(1)}, bf16[128,2048]{1,0:T...) custom-call(bf16[128,2048]{1,0:T(8,128)(2,1)} %q_hbm.1, bf16[128,2048]{1,0:T(8,128)(2,1)} %k_hbm.1, ...), custom_call_target="tpu_custom_call" | custom-call | tf_op jit(solution)/shard_map/packed_attention/pallas_call | solution.py:349
  105.5 1.4 %store.1 = (bf16[128,2048]{1,0:T(8,128)(2,1)}, bf16[128,2048]{1,0:T(8,128)(2,1)}, bf16[128,2048]{1,0:T(8,128)(2,1)}, bf16[128,2048]{1,0:T(8,128)(2,1)}, f32[16,128]{1,0:T(8,128)}, /*index=5*/f32[16,128]{1,0:T(8,128)}) custom-call(bf16[128,2048]{1,0:T(8,128)(2,1)S(1)} %get-tuple-element.18.refs_0_, bf16[128,2048]{1,0:T(8,128)(2,1)S(1)} %get-tuple-element.19.refs_1_, ...), custom_call_target="tpu_custom_call" | custom-call | tf_op jit(solution)/shard_map/store/pallas_call | solution.py:395

commit v3 on v2

--- a/solution.py
+++ b/solution.py
@@ -22,6 +22,7 @@
 SCALE = D_HEAD ** (-0.5)
 LOG2E = 1.4426950408889634
 SLOTS = 16
+ORDER = ((2, 0), (2, 1), (1, 0), (3, 0), (1, 1), (3, 1), (0, 1))
 
 
 def nt(a, b):
@@ -69,9 +70,11 @@
     def greet(device):
         pl.semaphore_signal(barrier, inc=1, device_id=device, device_id_type=MESH)
 
-    def member(step):
-        other = lax.rem(me + step, N_SEQ)
-        return other, {"seq_0": other // 2, "seq_1": lax.rem(other, 2)}
+    def member(hops, turn):
+        at, side = lax.rem(chip + hops, 4), lax.rem(core + turn, 2)
+        return at * 2 + side, {"seq_0": at, "seq_1": side}
+
+    members = [member(hops, turn) for hops, turn in ORDER]
 
     def across(step):
         other = lax.rem(ylo * N_SEQ + me + step, SLOTS)
@@ -85,8 +88,7 @@
     z_peers = [{"dp_1": lax.rem(z + d, 12)} for d in range(1, 12)]
     y_peers = [across(d) for d in range(1, SLOTS)]
     leaders = x_peers + z_peers + [{"dp_0": 1 - ylo}]
-    for step in range(1, N_SEQ):
-        other, device = member(step)
+    for other, device in members:
 
         @pl.when(other != 0)
         def _():
@@ -138,8 +140,7 @@
 
     for h in range(2):
         for a in range(4):
-            for step in (2, 3, 6, 7, 4, 5, 1):
-                other, device = member(step)
+            for other, device in members:
                 pltpu.make_async_remote_copy(
                     src_ref=sources[a].at[:, columns(other, h)],
                     dst_ref=rx.at[a, h, my_rows],
@@ -158,13 +159,19 @@
         piece = jnp.broadcast_to(key_row[:, j * 128 : (j + 1) * 128], (128, 128))
         code[j * 128 : (j + 1) * 128, :] = piece.T
 
+    @pl.when(leader)
+    def _():
+        pl.semaphore_wait(barrier, len(leaders))
+        for device in leaders:
+            pl.semaphore_signal(line, inc=1, device_id=device, device_id_type=MESH)
+
     def of_all(a, h, sends, recvs):
         return pltpu.make_async_remote_copy(
             src_ref=rx.at[a, h, pl.ds(0, 7 * ROWS)],
             dst_ref=rx.at[a, h, pl.ds(0, 7 * ROWS)],
             send_sem=sends.at[a, h],
             recv_sem=recvs.at[a, h],
-            device_id=member(1)[1],
+            device_id=members[0][1],
             device_id_type=MESH,
         )
 
@@ -181,8 +188,8 @@
         ).start()
 
     def send_all(a, h):
-        for step in (2, 3, 6, 7, 4, 5, 1):
-            send_out(a, h, member(step)[0])
+        for other, _ in members:
+            send_out(a, h, other)
 
     def keep_own(a, h):
         landing[a][:, columns(me, h)] = tx[a, h, my_rows, :]
@@ -238,8 +245,7 @@
         tx[2, h] = acc_k[...].astype(jnp.bfloat16)
         tx[3, h] = acc_v[...].astype(jnp.bfloat16)
         if h == 1:
-            for a in (2, 3):
-                send_all(a, h)
+            send_all(2, h)
         for a in range(4):
             keep_own(a, h)
         k_sum = jnp.sum(
@@ -249,9 +255,9 @@
 
             @pl.when(leader)
             def _():
-                pl.semaphore_wait(barrier, len(leaders))
-                for device in leaders:
-                    pl.semaphore_signal(line, inc=1, device_id=device, device_id_type=MESH)
+                pl.semaphore_wait(line, len(leaders))
+                for _, device in members:
+                    pl.semaphore_signal(go, inc=1, device_id=device, device_id_type=MESH)
 
         part[h : h + 1, :] = q_sum / qg_ref[pl.ds(me * 2 + h, 1), :]
         part[2 + h : 3 + h, :] = k_sum / kg_ref[pl.ds(me * 2 + h, 1), :]
@@ -272,12 +278,6 @@
         )
         copy.wait_recv()
         copy.wait_send()
-
-    @pl.when(leader)
-    def _():
-        pl.semaphore_wait(line, len(leaders))
-        for step in range(1, N_SEQ):
-            pl.semaphore_signal(go, inc=1, device_id=member(step)[1], device_id_type=MESH)
 
     @pl.when(me != 0)
     def _():
@@ -295,6 +295,7 @@
     slot = ylo * N_SEQ + me
     gy[slot] = total
     spread(gy.at[slot], y_peers, 2)
+    send_all(3, 1)
 
     def norm_back(raw_ref, inv_ref, gain, grads, out):
         def rows_of(i, _):

time: 108 us -> 105 us (0.972); the launches traced: 107 us -> 105 us
    pallas_call x1, Pallas kernels: 105 us -> 103 us  [per_device(): pl.pallas_call(kernel, out_shape=outs, in_specs=[hbm] * 8, out_specs=[vme...]
where the time goes in v3:
time: 105 us
  Pallas kernels  105 us (100%)
    pallas_call x1, Pallas kernels, per_device(): pl.pallas_call(kernel, out_shape=outs, in_specs=[hbm] * 8, out_specs=[vme...  103 us

profile of v3, /device:TPU:1, one launch (start us, length us, event | category | flops | bytes accessed | tf_op | source)
XLA Modules:
  0.0 105.2 jit_solution(1102770292238907066)
XLA Ops:
  0.6 103.1 %packed_attention.1 = (bf16[128,2048]{1,0:T(8,128)(2,1)S(1)}, bf16[128,2048]{1,0:T(8,128)(2,1)S(1)}, bf16[128,2048]{1,0:T(8,128)(2,1)S(1)}, bf16[128,2048]{1,0:T...) custom-call(bf16[128,2048]{1,0:T(8,128)(2,1)} %q_hbm.1, bf16[128,2048]{1,0:T(8,128)(2,1)} %k_hbm.1, ...), custom_call_target="tpu_custom_call" | custom-call | tf_op jit(solution)/shard_map/packed_attention/pallas_call | solution.py:350
  103.8 1.4 %store.1 = (bf16[128,2048]{1,0:T(8,128)(2,1)}, bf16[128,2048]{1,0:T(8,128)(2,1)}, bf16[128,2048]{1,0:T(8,128)(2,1)}, bf16[128,2048]{1,0:T(8,128)(2,1)}, f32[16,128]{1,0:T(8,128)}, /*index=5*/f32[16,128]{1,0:T(8,128)}) custom-call(bf16[128,2048]{1,0:T(8,128)(2,1)S(1)} %get-tuple-element.18.refs_0_, bf16[128,2048]{1,0:T(8,128)(2,1)S(1)} %get-tuple-element.19.refs_1_, ...), custom_call_target="tpu_custom_call" | custom-call | tf_op jit(solution)/shard_map/store/pallas_call | solution.py:396

commit v4 on v3

--- a/solution.py
+++ b/solution.py
@@ -110,7 +110,6 @@
 
         lax.fori_loop(0, ROWS // 16, rows_of, 0)
 
-    part[...] = jnp.zeros_like(part)
     loads[0].wait()
     loads[1].wait()
     q_gain = wide(qg_ref)
@@ -372,10 +371,10 @@
             pltpu.VMEM((LEN, 128), f32),
             pltpu.VMEM((LEN, D_HEAD), f32),
             pltpu.VMEM((LEN, D_HEAD), f32),
-            pltpu.VMEM((8, 128), f32),
-            pltpu.VMEM((4, 8, 128), f32),
-            pltpu.VMEM((12, 8, 128), f32),
-            pltpu.VMEM((SLOTS, 8, 128), f32),
+            pltpu.VMEM((4, 128), f32),
+            pltpu.VMEM((4, 4, 128), f32),
+            pltpu.VMEM((12, 4, 128), f32),
+            pltpu.VMEM((SLOTS, 4, 128), f32),
             dma((4, 2)), dma((4, 2)), dma((4, 2)), dma((4, 2)), dma((3,)), dma((3,)), dma((8,)),
             pltpu.SemaphoreType.REGULAR, pltpu.SemaphoreType.REGULAR, pltpu.SemaphoreType.REGULAR,
         ],

time: 105 us -> 105 us (level)
  no operation moved by 1% of the time
where the time goes in v4:
time: 105 us; the launch traced here: 104 us
  Pallas kernels  104 us (99%)
    pallas_call x1, Pallas kernels, per_device(): pl.pallas_call(kernel, out_shape=outs, in_specs=[hbm] * 8, out_specs=[vme...  102 us

profile of v4, /device:TPU:1, one launch (start us, length us, event | category | flops | bytes accessed | tf_op | source)
XLA Modules:
  0.0 104.4 jit_solution(13240357561726979489)
XLA Ops:
  0.6 102.4 %packed_attention.1 = (bf16[128,2048]{1,0:T(8,128)(2,1)S(1)}, bf16[128,2048]{1,0:T(8,128)(2,1)S(1)}, bf16[128,2048]{1,0:T(8,128)(2,1)S(1)}, bf16[128,2048]{1,0:T...) custom-call(bf16[128,2048]{1,0:T(8,128)(2,1)} %q_hbm.1, bf16[128,2048]{1,0:T(8,128)(2,1)} %k_hbm.1, ...), custom_call_target="tpu_custom_call" | custom-call | tf_op jit(solution)/shard_map/packed_attention/pallas_call | solution.py:349
  103.0 1.4 %store.1 = (bf16[128,2048]{1,0:T(8,128)(2,1)}, bf16[128,2048]{1,0:T(8,128)(2,1)}, bf16[128,2048]{1,0:T(8,128)(2,1)}, bf16[128,2048]{1,0:T(8,128)(2,1)}, f32[16,128]{1,0:T(8,128)}, /*index=5*/f32[16,128]{1,0:T(8,128)}) custom-call(bf16[128,2048]{1,0:T(8,128)(2,1)S(1)} %get-tuple-element.18.refs_0_, bf16[128,2048]{1,0:T(8,128)(2,1)S(1)} %get-tuple-element.19.refs_1_, ...), custom_call_target="tpu_custom_call" | custom-call | tf_op jit(solution)/shard_map/store/pallas_call | solution.py:395
